TPU v7x, 32 devices: a whole 2x2x4 slice. The times are simulated.
32 devices in a mesh: row: 8 (over z, y), basis: 4 (over x, core).
Axes of the slice: x: 2, y: 2, z: 4, core: 2. Of those that a mesh axis runs over, the one named last changes fastest.
Arguments:
- design: float32 [7680, 40960], P('row', 'basis'), may hold values from -0.029646354 to 0.029646354
- targets: float32 [7680], P('row'), may hold values from -6 to 6
- counts: int32 [7680, 128], P('row'), may hold values from 0 to 3
- coefficients: float32 [40960, 128], P('basis'), may hold values from -6 to 6
- step_size: float32 [128], replicated, may hold values from 0.03 to 0.15
Outputs:
- fitted: float32 [40960, 128], P('basis')
- influence: float32 [7680, 128], P('row')
All inputs are finite; a program needn't handle non-finite values.
Results may differ from a plain program's by a relative error of at most 0.00017.
Values sent between devices are 32-bit elements; how exact they have to be, the bound alone decides.
No kernel may reach another device: no remote copies, remote signals or barrier semaphores. Data moves between devices by JAX's collectives and lax.ppermute only.
A program may use at most 128 MiB of HBM per device.

v0:
```python
import jax
import jax.numpy as jnp
from jax import lax
from jax.sharding import PartitionSpec as P

STEPS = 3
HIGH = lax.Precision.HIGHEST


def transposed(left, right):
    return lax.dot_general(
        left, right, (((0,), (0,)), ((), ())), precision=HIGH, preferred_element_type=jnp.float32
    )


def predictions(partial_value):
    return lax.psum(partial_value, "basis")


def weighted(predicted, targets, weights):
    residual = predicted - targets[:, None]
    return weights * residual / jnp.sqrt(1.0 + residual * residual)


def shards(design, targets, counts, coefficients, step_size):
    weights = counts.astype(jnp.float32)
    curve_term = transposed(design * design, weights)
    influence = jnp.zeros((design.shape[0], coefficients.shape[1]), jnp.float32)
    share_rows = coefficients.shape[0] // lax.axis_size("row")
    offset = lax.axis_index("row") * share_rows
    curvature = lax.psum_scatter(curve_term, "row", scatter_dimension=0, tiled=True) + 0.01
    share = lax.dynamic_slice_in_dim(coefficients, offset, share_rows, 0)
    for step in range(STEPS):
        if step == 0:
            partial_value = jnp.dot(
                design, coefficients, precision=HIGH, preferred_element_type=jnp.float32
            )
        else:
            partial_value = jnp.dot(
                design,
                lax.all_gather(share, "row", axis=0, tiled=True),
                precision=HIGH,
                preferred_element_type=jnp.float32,
            )
        influence = weighted(predictions(partial_value), targets, weights)
        gradient = lax.psum_scatter(
            transposed(design, influence), "row", scatter_dimension=0, tiled=True
        )
        share = share - step_size[None, :] * gradient / curvature
    fitted = lax.all_gather(share, "row", axis=0, tiled=True)
    return (fitted, influence)


def solution(mesh):
    return jax.shard_map(
        shards,
        mesh=mesh,
        in_specs=(P("row", "basis"), P("row"), P("row", None), P("basis", None), P()),
        out_specs=(P("basis", None), P("row", None)),
        check_vma=False,
    )
```

profile of v0, /device:TPU:0, one launch (start us, length us, event | category | flops | bytes accessed | tf_op | source)
XLA Modules:
  0.0 961.2 jit_solution(473307508805316564)
XLA Ops:
  8.0 0.0 copy-start
  8.0 0.0 all-reduce.4.cloned.1.call-start
  8.1 35.6 %fusion.23 = f32[960,128]{1,0:T(8,128)} fusion(f32[960,10240]{1,0:T(8,128)} %param.5, f32[10240,128]{1,0:T(8,128)} %param.8), kind=kOutput, calls=%fused_computation.33 | convolution fusion | flops 15099494400 | bytes 45056000 | tf_op jit(solution)/shard_map/dot_general | solution.py:35
  43.6 0.0 all-reduce.4.cloned.1.call-update
  43.6 0.0 reduce-scatter.7.cloned.1.call-start
  43.7 29.3 %fusion = f32[10240,128]{0,1:T(8,128)} fusion(f32[960,10240]{1,0:T(8,128)} %param.5, s32[960,128]{1,0:T(8,128)S(1)} %copy-done), kind=kOutput, calls=%fused_computation | convolution fusion | flops 15109447680 | bytes 45056000 | tf_op jit(solution)/shard_map/dot_general | solution.py:11
  73.0 0.0 reduce-scatter.7.cloned.1.call-update
  73.1 0.0 copy-start.6
  73.1 0.6 reduce-scatter.5.cloned.1.call-start
  73.6 6.2 all-reduce.4.cloned.1.call-done
  79.8 29.3 %convolution_bitcast_fusion.2 = f32[10240,128]{0,1:T(8,128)} fusion(f32[960,10240]{1,0:T(8,128)} %param.5, f32[960,128]{1,0:T(8,128)} %all-reduce.4.cloned.1.call-done, s32[960,128]{1,0:T(8,128)S(1)} %copy-done, f32[960]{0:T(1024)S(1)} %copy-done.5), kind=kOutput, calls=%fused_computation.4 | convolution fusion | flops 15100231680 | bytes 45551360 | tf_op jit(solution)/shard_map/dot_general | solution.py:11
  109.1 0.0 reduce-scatter.5.cloned.1.call-update
  109.1 0.0 all-gather.4.cloned.1.call-start
  109.2 1.1 constant_dynamic-slice_fusion
  110.3 0.2 copy.11
  110.6 68.3 %reduce-scatter.7.cloned.1.call-done = f32[1280,128]{0,1:T(8,128)} async-done(((f32[10240,128]{0,1:T(8,128)}), f32[1280,128]{0,1:T(8,128)}) %reduce-scatter.7.cloned.1.call-update) | async-done | bytes 655376 | tf_op jit(solution)/shard_map/reduce_scatter | solution.py:31
  178.9 106.6 %reduce-scatter.5.cloned.1.call-done = f32[1280,128]{0,1:T(8,128)} async-done(((f32[10240,128]{0,1:T(8,128)}), f32[1280,128]{0,1:T(8,128)}) %reduce-scatter.5.cloned.1.call-update) | async-done | bytes 655376 | tf_op jit(solution)/shard_map/reduce_scatter | solution.py:46
  285.5 2.3 divide_subtract_fusion.2
  287.8 0.0 all-gather.4.cloned.1.call-update
  287.8 0.2 all-reduce.6.cloned.1.call-start
  288.0 85.1 %all-gather.4.cloned.1.call-done = f32[10240,128]{0,1:T(8,128)} async-done(((f32[1280,128]{0,1:T(8,128)}), f32[10240,128]{0,1:T(8,128)}) %all-gather.4.cloned.1.call-update) | async-done | bytes 5242896 | tf_op jit(solution)/shard_map/all_gather | solution.py:41
  373.2 35.7 %convolution_bitcast_fusion.4 = f32[960,128]{1,0:T(8,128)} fusion(f32[10240,128]{0,1:T(8,128)} %all-gather.4.cloned.1.call-done, f32[960,10240]{1,0:T(8,128)} %param.5), kind=kOutput, calls=%fused_computation.6 | convolution fusion | flops 15099494400 | bytes 45056000 | tf_op jit(solution)/shard_map/dot_general | solution.py:39
  408.8 0.0 all-reduce.6.cloned.1.call-update
  408.8 0.3 reduce-scatter.9.cloned.1.call-start
  409.1 31.5 %all-reduce.6.cloned.1.call-done = f32[960,128]{1,0:T(8,128)} async-done(((f32[960,128]{1,0:T(8,128)}), f32[960,128]{1,0:T(8,128)}) %all-reduce.6.cloned.1.call-update) | async-done | bytes 491536 | tf_op jit(solution)/shard_map/psum | solution.py:17
  440.6 29.0 %convolution_bitcast_fusion.1 = f32[10240,128]{0,1:T(8,128)} fusion(f32[960,10240]{1,0:T(8,128)} %param.5, f32[960,128]{1,0:T(8,128)} %all-reduce.6.cloned.1.call-done, s32[960,128]{1,0:T(8,128)S(1)} %copy-done, f32[960]{0:T(1024)S(1)} %copy-done.5), kind=kOutput, calls=%fused_computation.3 | convolution fusion | flops 15100231680 | bytes 45551360 | tf_op jit(solution)/shard_map/dot_general | solution.py:11
  469.6 0.0 reduce-scatter.9.cloned.1.call-update
  469.6 0.0 all-gather.6.cloned.1.call-start
  469.6 103.1 %reduce-scatter.9.cloned.1.call-done = f32[1280,128]{0,1:T(8,128)} async-done(((f32[10240,128]{0,1:T(8,128)}), f32[1280,128]{0,1:T(8,128)}) %reduce-scatter.9.cloned.1.call-update) | async-done | bytes 655376 | tf_op jit(solution)/shard_map/reduce_scatter | solution.py:46
  572.7 0.0 copy-done.3
  572.7 2.1 divide_subtract_fusion.1
  574.8 0.0 all-gather.6.cloned.1.call-update
  574.9 0.3 all-reduce.8.cloned.1.call-start
  575.2 85.0 %all-gather.6.cloned.1.call-done = f32[10240,128]{0,1:T(8,128)} async-done(((f32[1280,128]{0,1:T(8,128)}), f32[10240,128]{0,1:T(8,128)}) %all-gather.6.cloned.1.call-update) | async-done | bytes 5242896 | tf_op jit(solution)/shard_map/all_gather | solution.py:41
  660.2 35.7 %convolution_bitcast_fusion.3 = f32[960,128]{1,0:T(8,128)} fusion(f32[10240,128]{0,1:T(8,128)} %all-gather.6.cloned.1.call-done, f32[960,10240]{1,0:T(8,128)} %param.5), kind=kOutput, calls=%fused_computation.5 | convolution fusion | flops 15099494400 | bytes 45056000 | tf_op jit(solution)/shard_map/dot_general | solution.py:39
  695.8 0.0 all-reduce.8.cloned.1.call-update
  695.9 0.3 reduce-scatter.11.cloned.1.call-start
  696.2 31.4 %all-reduce.8.cloned.1.call-done = f32[960,128]{1,0:T(8,128)} async-done(((f32[960,128]{1,0:T(8,128)}), f32[960,128]{1,0:T(8,128)}) %all-reduce.8.cloned.1.call-update) | async-done | bytes 491536 | tf_op jit(solution)/shard_map/psum | solution.py:17
  727.6 1.2 rsqrt_multiply_fusion
  728.8 0.0 copy-start.4
  728.9 27.8 %convolution_bitcast_fusion = f32[10240,128]{0,1:T(8,128)} fusion(f32[960,128]{1,0:T(8,128)S(1)} %rsqrt_multiply_fusion, f32[960,10240]{1,0:T(8,128)} %param.5), kind=kOutput, calls=%fused_computation.2 | convolution fusion | flops 15099494400 | bytes 45056000 | tf_op jit(solution)/shard_map/dot_general | solution.py:11
  756.7 0.0 reduce-scatter.11.cloned.1.call-update
  756.7 0.0 all-gather.8.cloned.1.call-start
  756.8 103.1 %reduce-scatter.11.cloned.1.call-done = f32[1280,128]{0,1:T(8,128)} async-done(((f32[10240,128]{0,1:T(8,128)}), f32[1280,128]{0,1:T(8,128)}) %reduce-scatter.11.cloned.1.call-update) | async-done | bytes 655376 | tf_op jit(solution)/shard_map/reduce_scatter | solution.py:46
  859.8 2.1 divide_subtract_fusion
  861.9 0.0 all-gather.8.cloned.1.call-update
  861.9 85.8 %all-gather.8.cloned.1.call-done = f32[10240,128]{0,1:T(8,128)} async-done(((f32[1280,128]{0,1:T(8,128)}), f32[10240,128]{0,1:T(8,128)}) %all-gather.8.cloned.1.call-update) | async-done | bytes 5242896 | tf_op jit(solution)/shard_map/all_gather | solution.py:50
  947.7 5.9 copy.9
  (10 shorter events, 0.0 us)
Async XLA Ops:
  8.0 35.7 %copy-start = (s32[960,128]{1,0:T(8,128)S(1)}, s32[960,128]{1,0:T(8,128)}, u32[]{:S(2)}) copy-start(s32[960,128]{1,0:T(8,128)} %param.7) | copy-start | bytes 1474564
  8.0 71.8 %all-reduce.4.cloned.1.call-start = ((), (), s32[]{:S(2)}) async-start(), calls=%async_computation.4 | async-start | bytes 983040 | tf_op jit(solution)/shard_map/psum | solution.py:17
  43.6 36.2 %copy-start.5 = (f32[960]{0:T(1024)S(1)}, f32[960]{0:T(1024)}, u32[]{:S(2)}) copy-start(f32[960]{0:T(1024)} %param.6) | copy-start | bytes 11524
  43.6 135.2 %reduce-scatter.7.cloned.1.call-start = ((), (), s32[]{:S(2)}) async-start(), calls=%async_computation.6 | async-start | bytes 5898240 | tf_op jit(solution)/shard_map/reduce_scatter | solution.py:31
  73.1 212.4 %copy-start.6 = (f32[128]{0:T(128)S(1)}, f32[128]{0:T(128)}, u32[]{:S(2)}) copy-start(f32[128]{0:T(128)} %param.9) | copy-start | bytes 1540
  73.1 212.4 %reduce-scatter.5.cloned.1.call-start = ((), (), s32[]{:S(2)}) async-start(), calls=%async_computation.5 | async-start | bytes 5898240 | tf_op jit(solution)/shard_map/reduce_scatter | solution.py:46
  109.1 264.0 %all-gather.4.cloned.1.call-start = ((), (), s32[]{:S(2)}) async-start(), calls=%async_computation.7 | async-start | bytes 5898240 | tf_op jit(solution)/shard_map/all_gather | solution.py:41
  287.8 152.8 %all-reduce.6.cloned.1.call-start = ((), (), s32[]{:S(2)}) async-start(), calls=%async_computation.8 | async-start | bytes 983040 | tf_op jit(solution)/shard_map/psum | solution.py:17
  408.8 163.9 %copy-start.2 = (f32[1280,128]{0,1:T(8,128)S(1)}, f32[1280,128]{0,1:T(8,128)}, u32[]{:S(2)}) copy-start(f32[1280,128]{0,1:T(8,128)} %divide_subtract_fusion.2) | copy-start | bytes 1966084
  408.8 163.9 %copy-start.3 = (f32[1280,128]{0,1:T(8,128)S(1)}, f32[1280,128]{0,1:T(8,128)}, u32[]{:S(2)}) copy-start(f32[1280,128]{0,1:T(8,128)} %reduce-scatter.7.cloned.1.call-done) | copy-start | bytes 1966084
  408.8 163.9 %reduce-scatter.9.cloned.1.call-start = ((), (), s32[]{:S(2)}) async-start(), calls=%async_computation.9 | async-start | bytes 5898240 | tf_op jit(solution)/shard_map/reduce_scatter | solution.py:46
  469.6 190.6 %all-gather.6.cloned.1.call-start = ((), (), s32[]{:S(2)}) async-start(), calls=%async_computation.10 | async-start | bytes 5898240 | tf_op jit(solution)/shard_map/all_gather | solution.py:41
  574.9 152.8 %all-reduce.8.cloned.1.call-start = ((), (), s32[]{:S(2)}) async-start(), calls=%async_computation.11 | async-start | bytes 983040 | tf_op jit(solution)/shard_map/psum | solution.py:17
  695.8 164.0 %copy-start.1 = (f32[1280,128]{0,1:T(8,128)S(1)}, f32[1280,128]{0,1:T(8,128)}, u32[]{:S(2)}) copy-start(f32[1280,128]{0,1:T(8,128)} %divide_subtract_fusion.1) | copy-start | bytes 1966084
  695.9 163.9 %reduce-scatter.11.cloned.1.call-start = ((), (), s32[]{:S(2)}) async-start(), calls=%async_computation.12 | async-start | bytes 5898240 | tf_op jit(solution)/shard_map/reduce_scatter | solution.py:46
  728.8 224.7 %copy-start.4 = (f32[960,128]{1,0:T(8,128)}, f32[960,128]{1,0:T(8,128)S(1)}, u32[]{:S(2)}) copy-start(f32[960,128]{1,0:T(8,128)S(1)} %rsqrt_multiply_fusion) | copy-start | bytes 1474564
  756.7 191.0 %all-gather.8.cloned.1.call-start = ((), (), s32[]{:S(2)}) async-start(), calls=%async_computation.13 | async-start | bytes 5898240 | tf_op jit(solution)/shard_map/all_gather | solution.py:50
Sparse Core Ops, SparseCore 0:
  43.8 36.0 all-reduce.3
  409.0 31.5 all-reduce.5
  696.0 31.5 all-reduce.7
Sparse Core Ops, SparseCore 1:
  73.1 105.7 reduce-scatter.6
  182.9 102.5 reduce-scatter.4
  287.9 85.2 all-gather.3
  469.7 103.0 reduce-scatter.8
  574.9 85.2 all-gather.5
  756.8 103.0 reduce-scatter.10
  862.5 85.2 all-gather.7
where the time goes:
time: 969 us; the launch traced here: 961 us
  waiting for transfers between devices  706 us (73%)
  matrix products  222 us (23%)
  between operations  15.9 us (2%)
    reduce_scatter x3, waiting for transfers between devices, shards(): lax.psum_scatter(transposed(design, influence), 'row', scatter_dimension=...  313 us
    all_gather x2, waiting for transfers between devices, shards(): lax.all_gather(share, 'row', axis=0, tiled=True)  170 us
    dot_general x4, matrix products, transposed(): lax.dot_general(left, right, (((0,), (0,)), ((), ())), precision=HIGH, pr...  115 us
    all_gather x1, waiting for transfers between devices, shards(): fitted = lax.all_gather(share, 'row', axis=0, tiled=True)  85.8 us
    dot_general x2, matrix products, shards(): jnp.dot(design, lax.all_gather(share, 'row', axis=0, tiled=True), precisi...  71.3 us
    psum x3, waiting for transfers between devices, predictions(): return lax.psum(partial_value, 'basis')  69 us
    reduce_scatter x1, waiting for transfers between devices, shards(): lax.psum_scatter(curve_term, 'row', scatter_dimension=0, tiled=True) + 0.01  68.3 us
    dot_general x1, matrix products, shards(): jnp.dot(design, coefficients, precision=HIGH, preferred_element_type=jnp....  35.6 us
  transfers between devices with their start and end apart: 10, of which 10 were waited for; matrix products, arithmetic and copies ran while one was open for 6% of the time, Pallas kernels for 0%

commit v1 on v0

--- a/solution.py
+++ b/solution.py
@@ -23,6 +23,19 @@
 
 
 def shards(design, targets, counts, coefficients, step_size):
+
+    def _play_runs(target):
+        mesh_ax = "row"
+        nodes = lax.axis_size(mesh_ax)
+        f_next = [None] * nodes
+        pool = [(w, (w + 1) % nodes) for w in range(nodes)]
+        f_next[nodes - 1] = target
+        for j in range(nodes - 2, -1, -1):
+            f_next[j] = lax.ppermute(f_next[j + 1], mesh_ax, pool)
+        view_out = jnp.concatenate(f_next, axis=0)
+        mid_arr = jnp.roll(view_out, (lax.axis_index(mesh_ax) + 1) * target.shape[0], axis=0)
+        return mid_arr
+
     weights = counts.astype(jnp.float32)
     curve_term = transposed(design * design, weights)
     influence = jnp.zeros((design.shape[0], coefficients.shape[1]), jnp.float32)
@@ -47,7 +60,7 @@
             transposed(design, influence), "row", scatter_dimension=0, tiled=True
         )
         share = share - step_size[None, :] * gradient / curvature
-    fitted = lax.all_gather(share, "row", axis=0, tiled=True)
+    fitted = _play_runs(share)
     return (fitted, influence)
 
 

time: 969 us -> 1010 us (1.042)
  waiting for transfers between devices: 706 us -> 733 us
  local copies, waits for them, and re-layouts: 7.27 us -> 20.3 us
    ppermute x0 -> x7, waiting for transfers between devices: none -> 112 us  [_play_runs(): f_next[j] = lax.ppermute(f_next[j + 1], mesh_ax, pool)]
    all_gather x1 -> x0, waiting for transfers between devices: 85.8 us -> none  [shards(): fitted = lax.all_gather(share, 'row', axis=0, tiled=True)]
  transfers between devices with their start and end apart: 10 -> 16, of which waited for: 10 -> 16; matrix products, arithmetic and copies ran while one was open for 6% -> 6% of each run, Pallas kernels for 0% -> 0%
where the time goes in v1:
time: 1010 us; the launch traced here: 1000 us
  waiting for transfers between devices  733 us (73%)
  matrix products  222 us (22%)
  local copies, waits for them, and re-layouts  20.3 us (2%)
  between operations  15.7 us (2%)
    reduce_scatter x3, waiting for transfers between devices, shards(): lax.psum_scatter(transposed(design, influence), 'row', scatter_dimension=...  313 us
    all_gather x2, waiting for transfers between devices, shards(): lax.all_gather(share, 'row', axis=0, tiled=True)  170 us
    dot_general x4, matrix products, transposed(): lax.dot_general(left, right, (((0,), (0,)), ((), ())), precision=HIGH, pr...  115 us
    ppermute x7, waiting for transfers between devices, _play_runs(): f_next[j] = lax.ppermute(f_next[j + 1], mesh_ax, pool)  112 us
    dot_general x2, matrix products, shards(): jnp.dot(design, lax.all_gather(share, 'row', axis=0, tiled=True), precisi...  71.3 us
    psum x3, waiting for transfers between devices, predictions(): return lax.psum(partial_value, 'basis')  69.6 us
    reduce_scatter x1, waiting for transfers between devices, shards(): lax.psum_scatter(curve_term, 'row', scatter_dimension=0, tiled=True) + 0.01  68.2 us
    dot_general x1, matrix products, shards(): jnp.dot(design, coefficients, precision=HIGH, preferred_element_type=jnp....  35.6 us
  transfers between devices with their start and end apart: 16, of which 16 were waited for; matrix products, arithmetic and copies ran while one was open for 6% of the time, Pallas kernels for 0%

profile of v1, /device:TPU:0, one launch (start us, length us, event | category | flops | bytes accessed | tf_op | source)
XLA Modules:
  0.0 1001.1 jit_solution(9278459644424200290)
XLA Ops:
  8.1 35.6 %fusion.23 = f32[960,128]{1,0:T(8,128)} fusion(f32[960,10240]{1,0:T(8,128)} %param.5, f32[10240,128]{1,0:T(8,128)} %param.8), kind=kOutput, calls=%fused_computation.50 | convolution fusion | flops 15099494400 | bytes 45056000 | tf_op jit(solution)/shard_map/dot_general | solution.py:48
  43.7 29.3 %fusion = f32[10240,128]{0,1:T(8,128)} fusion(f32[960,10240]{1,0:T(8,128)} %param.5, s32[960,128]{1,0:T(8,128)S(1)} %copy-done), kind=kOutput, calls=%fused_computation | convolution fusion | flops 15109447680 | bytes 45056000 | tf_op jit(solution)/shard_map/dot_general | solution.py:11
  73.1 0.2 reduce-scatter.5.cloned.1.call-start
  73.3 6.6 all-reduce.4.cloned.1.call-done
  79.9 29.3 %convolution_bitcast_fusion.2 = f32[10240,128]{0,1:T(8,128)} fusion(f32[960,10240]{1,0:T(8,128)} %param.5, f32[960,128]{1,0:T(8,128)} %all-reduce.4.cloned.1.call-done, s32[960,128]{1,0:T(8,128)S(1)} %copy-done, f32[960]{0:T(1024)S(1)} %copy-done.9), kind=kOutput, calls=%fused_computation.4 | convolution fusion | flops 15100231680 | bytes 45551360 | tf_op jit(solution)/shard_map/dot_general | solution.py:11
  109.2 1.1 constant_dynamic-slice_fusion.1
  110.4 0.2 copy.11
  110.6 68.2 %reduce-scatter.7.cloned.1.call-done = f32[1280,128]{0,1:T(8,128)} async-done(((f32[10240,128]{0,1:T(8,128)}), f32[1280,128]{0,1:T(8,128)}) %reduce-scatter.7.cloned.1.call-update) | async-done | bytes 655376 | tf_op jit(solution)/shard_map/reduce_scatter | solution.py:44
  178.8 106.6 %reduce-scatter.5.cloned.1.call-done = f32[1280,128]{0,1:T(8,128)} async-done(((f32[10240,128]{0,1:T(8,128)}), f32[1280,128]{0,1:T(8,128)}) %reduce-scatter.5.cloned.1.call-update) | async-done | bytes 655376 | tf_op jit(solution)/shard_map/reduce_scatter | solution.py:59
  285.4 2.3 divide_subtract_fusion.2
  287.8 0.3 all-reduce.6.cloned.1.call-start
  288.0 85.1 %all-gather.3.cloned.1.call-done = f32[10240,128]{0,1:T(8,128)} async-done(((f32[1280,128]{0,1:T(8,128)}), f32[10240,128]{0,1:T(8,128)}) %all-gather.3.cloned.1.call-update) | async-done | bytes 5242896 | tf_op jit(solution)/shard_map/all_gather | solution.py:54
  373.1 35.6 %convolution_bitcast_fusion.4 = f32[960,128]{1,0:T(8,128)} fusion(f32[10240,128]{0,1:T(8,128)} %all-gather.3.cloned.1.call-done, f32[960,10240]{1,0:T(8,128)} %param.5), kind=kOutput, calls=%fused_computation.6 | convolution fusion | flops 15099494400 | bytes 45056000 | tf_op jit(solution)/shard_map/dot_general | solution.py:52
  408.8 0.3 reduce-scatter.9.cloned.1.call-start
  409.1 31.4 %all-reduce.6.cloned.1.call-done = f32[960,128]{1,0:T(8,128)} async-done(((f32[960,128]{1,0:T(8,128)}), f32[960,128]{1,0:T(8,128)}) %all-reduce.6.cloned.1.call-update) | async-done | bytes 491536 | tf_op jit(solution)/shard_map/psum | solution.py:17
  440.6 29.0 %convolution_bitcast_fusion.1 = f32[10240,128]{0,1:T(8,128)} fusion(f32[960,10240]{1,0:T(8,128)} %param.5, f32[960,128]{1,0:T(8,128)} %all-reduce.6.cloned.1.call-done, s32[960,128]{1,0:T(8,128)S(1)} %copy-done, f32[960]{0:T(1024)S(1)} %copy-done.9), kind=kOutput, calls=%fused_computation.3 | convolution fusion | flops 15100231680 | bytes 45551360 | tf_op jit(solution)/shard_map/dot_general | solution.py:11
  469.6 103.1 %reduce-scatter.9.cloned.1.call-done = f32[1280,128]{0,1:T(8,128)} async-done(((f32[10240,128]{0,1:T(8,128)}), f32[1280,128]{0,1:T(8,128)}) %reduce-scatter.9.cloned.1.call-update) | async-done | bytes 655376 | tf_op jit(solution)/shard_map/reduce_scatter | solution.py:59
  572.7 2.1 divide_subtract_fusion.1
  574.8 0.5 all-reduce.8.cloned.1.call-start
  575.4 84.8 %all-gather.5.cloned.1.call-done = f32[10240,128]{0,1:T(8,128)} async-done(((f32[1280,128]{0,1:T(8,128)}), f32[10240,128]{0,1:T(8,128)}) %all-gather.5.cloned.1.call-update) | async-done | bytes 5242896 | tf_op jit(solution)/shard_map/all_gather | solution.py:54
  660.2 35.6 %convolution_bitcast_fusion.3 = f32[960,128]{1,0:T(8,128)} fusion(f32[10240,128]{0,1:T(8,128)} %all-gather.5.cloned.1.call-done, f32[960,10240]{1,0:T(8,128)} %param.5), kind=kOutput, calls=%fused_computation.5 | convolution fusion | flops 15099494400 | bytes 45056000 | tf_op jit(solution)/shard_map/dot_general | solution.py:52
  695.9 0.2 reduce-scatter.11.cloned.1.call-start
  696.1 31.5 %all-reduce.8.cloned.1.call-done = f32[960,128]{1,0:T(8,128)} async-done(((f32[960,128]{1,0:T(8,128)}), f32[960,128]{1,0:T(8,128)}) %all-reduce.8.cloned.1.call-update) | async-done | bytes 491536 | tf_op jit(solution)/shard_map/psum | solution.py:17
  727.6 1.2 rsqrt_multiply_fusion
  728.9 27.9 %convolution_bitcast_fusion = f32[10240,128]{0,1:T(8,128)} fusion(f32[960,128]{1,0:T(8,128)S(1)} %rsqrt_multiply_fusion, f32[960,10240]{1,0:T(8,128)} %param.5), kind=kOutput, calls=%fused_computation.2 | convolution fusion | flops 15099494400 | bytes 45056000 | tf_op jit(solution)/shard_map/dot_general | solution.py:11
  756.8 103.1 %reduce-scatter.11.cloned.1.call-done = f32[1280,128]{0,1:T(8,128)} async-done(((f32[10240,128]{0,1:T(8,128)}), f32[1280,128]{0,1:T(8,128)}) %reduce-scatter.11.cloned.1.call-update) | async-done | bytes 655376 | tf_op jit(solution)/shard_map/reduce_scatter | solution.py:59
  859.9 1.3 divide_subtract_fusion
  861.2 1.5 collective-permute-start
  862.7 17.2 %collective-permute-done = f32[1280,128]{0,1:T(8,128)S(1)} collective-permute-done((f32[1280,128]{0,1:T(8,128)S(1)}, f32[1280,128]{0,1:T(8,128)S(1)}, u32[]{:S(2)}, u32[]{:S(2)}) %collective-permute-start) | collective-permute-done | bytes 655392 | tf_op jit(solution)/shard_map/ppermute | solution.py:34
  879.9 17.9 %collective-permute-done.1 = f32[1280,128]{0,1:T(8,128)S(1)} collective-permute-done((f32[1280,128]{0,1:T(8,128)S(1)}, f32[1280,128]{0,1:T(8,128)S(1)}, u32[]{:S(2)}, u32[]{:S(2)}) %collective-permute-start.1) | collective-permute-done | bytes 655392 | tf_op jit(solution)/shard_map/ppermute | solution.py:34
  897.8 17.0 %collective-permute-done.2 = f32[1280,128]{0,1:T(8,128)S(1)} collective-permute-done((f32[1280,128]{0,1:T(8,128)S(1)}, f32[1280,128]{0,1:T(8,128)S(1)}, u32[]{:S(2)}, u32[]{:S(2)}) %collective-permute-start.2) | collective-permute-done | bytes 655392 | tf_op jit(solution)/shard_map/ppermute | solution.py:34
  914.8 16.1 %collective-permute-done.3 = f32[1280,128]{0,1:T(8,128)S(1)} collective-permute-done((f32[1280,128]{0,1:T(8,128)S(1)}, f32[1280,128]{0,1:T(8,128)S(1)}, u32[]{:S(2)}, u32[]{:S(2)}) %collective-permute-start.3) | collective-permute-done | bytes 655392 | tf_op jit(solution)/shard_map/ppermute | solution.py:34
  930.9 0.9 copy-done.5
  931.8 15.3 %collective-permute-done.4 = f32[1280,128]{0,1:T(8,128)S(1)} collective-permute-done((f32[1280,128]{0,1:T(8,128)S(1)}, f32[1280,128]{0,1:T(8,128)S(1)}, u32[]{:S(2)}, u32[]{:S(2)}) %collective-permute-start.4) | collective-permute-done | bytes 655392 | tf_op jit(solution)/shard_map/ppermute | solution.py:34
  947.1 0.8 copy-done.7
  947.9 14.7 %collective-permute-done.5 = f32[1280,128]{0,1:T(8,128)} collective-permute-done((f32[1280,128]{0,1:T(8,128)S(1)}, f32[1280,128]{0,1:T(8,128)}, u32[]{:S(2)}, u32[]{:S(2)}) %collective-permute-start.5) | collective-permute-done | bytes 655392 | tf_op jit(solution)/shard_map/ppermute | solution.py:34
  962.6 13.9 %collective-permute-done.6 = f32[1280,128]{0,1:T(8,128)} collective-permute-done((f32[1280,128]{0,1:T(8,128)}, f32[1280,128]{0,1:T(8,128)}, u32[]{:S(2)}, u32[]{:S(2)}) %collective-permute-start.6) | collective-permute-done | bytes 655392 | tf_op jit(solution)/shard_map/ppermute | solution.py:34
  976.5 1.1 constant_dynamic-update-slice_fusion.15
  977.6 1.1 constant_dynamic-update-slice_fusion.14
  978.8 1.1 constant_dynamic-update-slice_fusion.13
  979.9 1.1 constant_dynamic-update-slice_fusion.12
  981.3 0.1 constant_dynamic-update-slice_fusion.8
  981.4 1.1 constant_dynamic-update-slice_fusion.7
  982.5 1.1 constant_dynamic-update-slice_fusion.6
  983.8 0.1 constant_dynamic-update-slice_fusion.3
  984.1 0.1 constant_dynamic-update-slice_fusion
  984.1 3.8 constant_dynamic-slice_fusion
  987.9 5.9 copy.9
  (46 shorter events, 0.8 us)
Async XLA Ops:
  8.0 35.7 %copy-start = (s32[960,128]{1,0:T(8,128)S(1)}, s32[960,128]{1,0:T(8,128)}, u32[]{:S(2)}) copy-start(s32[960,128]{1,0:T(8,128)} %param.7) | copy-start | bytes 1474564
  8.0 71.9 %all-reduce.4.cloned.1.call-start = ((), (), s32[]{:S(2)}) async-start(), calls=%async_computation.4 | async-start | bytes 983040 | tf_op jit(solution)/shard_map/psum | solution.py:17
  43.6 36.2 %copy-start.9 = (f32[960]{0:T(1024)S(1)}, f32[960]{0:T(1024)}, u32[]{:S(2)}) copy-start(f32[960]{0:T(1024)} %param.6) | copy-start | bytes 11524
  43.6 135.2 %reduce-scatter.7.cloned.1.call-start = ((), (), s32[]{:S(2)}) async-start(), calls=%async_computation.6 | async-start | bytes 5898240 | tf_op jit(solution)/shard_map/reduce_scatter | solution.py:44
  73.1 212.4 %copy-start.10 = (f32[128]{0:T(128)S(1)}, f32[128]{0:T(128)}, u32[]{:S(2)}) copy-start(f32[128]{0:T(128)} %param.9) | copy-start | bytes 1540
  73.1 212.4 %reduce-scatter.5.cloned.1.call-start = ((), (), s32[]{:S(2)}) async-start(), calls=%async_computation.5 | async-start | bytes 5898240 | tf_op jit(solution)/shard_map/reduce_scatter | solution.py:59
  109.2 263.9 %all-gather.3.cloned.1.call-start = ((), (), s32[]{:S(2)}) async-start(), calls=%async_computation.7 | async-start | bytes 5898240 | tf_op jit(solution)/shard_map/all_gather | solution.py:54
  287.8 152.8 %all-reduce.6.cloned.1.call-start = ((), (), s32[]{:S(2)}) async-start(), calls=%async_computation.8 | async-start | bytes 983040 | tf_op jit(solution)/shard_map/psum | solution.py:17
  408.8 163.9 %copy-start.1 = (f32[1280,128]{0,1:T(8,128)S(1)}, f32[1280,128]{0,1:T(8,128)}, u32[]{:S(2)}) copy-start(f32[1280,128]{0,1:T(8,128)} %divide_subtract_fusion.2) | copy-start | bytes 1966084
  408.8 163.9 %copy-start.3 = (f32[1280,128]{0,1:T(8,128)S(1)}, f32[1280,128]{0,1:T(8,128)}, u32[]{:S(2)}) copy-start(f32[1280,128]{0,1:T(8,128)} %reduce-scatter.7.cloned.1.call-done) | copy-start | bytes 1966084
  408.8 163.9 %reduce-scatter.9.cloned.1.call-start = ((), (), s32[]{:S(2)}) async-start(), calls=%async_computation.9 | async-start | bytes 5898240 | tf_op jit(solution)/shard_map/reduce_scatter | solution.py:59
  469.6 190.6 %all-gather.5.cloned.1.call-start = ((), (), s32[]{:S(2)}) async-start(), calls=%async_computation.10 | async-start | bytes 5898240 | tf_op jit(solution)/shard_map/all_gather | solution.py:54
  574.8 152.8 %all-reduce.8.cloned.1.call-start = ((), (), s32[]{:S(2)}) async-start(), calls=%async_computation.11 | async-start | bytes 983040 | tf_op jit(solution)/shard_map/psum | solution.py:17
  695.9 164.0 %reduce-scatter.11.cloned.1.call-start = ((), (), s32[]{:S(2)}) async-start(), calls=%async_computation.12 | async-start | bytes 5898240 | tf_op jit(solution)/shard_map/reduce_scatter | solution.py:59
  728.9 27.9 %copy-start.4 = (f32[960,128]{1,0:T(8,128)}, f32[960,128]{1,0:T(8,128)S(1)}, u32[]{:S(2)}) copy-start(f32[960,128]{1,0:T(8,128)S(1)} %rsqrt_multiply_fusion) | copy-start | bytes 1474564
  728.9 131.0 %copy-start.2 = (f32[1280,128]{0,1:T(8,128)S(1)}, f32[1280,128]{0,1:T(8,128)}, u32[]{:S(2)}) copy-start(f32[1280,128]{0,1:T(8,128)} %divide_subtract_fusion.1) | copy-start | bytes 1966084
  861.2 18.8 %collective-permute-start = (f32[1280,128]{0,1:T(8,128)S(1)}, f32[1280,128]{0,1:T(8,128)S(1)}, u32[]{:S(2)}, u32[]{:S(2)}) collective-permute-start(f32[1280,128]{0,1:T(8,128)S(1)} %divide_subtract_fusion), channel_id=1, source_target_pairs={{0,4},{4,8},{8,12},{12,16},{16,20},{20,24},{24,28},{28,0},{1,5},{5... | collective-permute-start | bytes 1966088 | tf_op jit(solution)/shard_map/ppermute | solution.py:34
  879.9 17.9 %collective-permute-start.1 = (f32[1280,128]{0,1:T(8,128)S(1)}, f32[1280,128]{0,1:T(8,128)S(1)}, u32[]{:S(2)}, u32[]{:S(2)}) collective-permute-start(f32[1280,128]{0,1:T(8,128)S(1)} %collective-permute-done), channel_id=1, source_target_pairs={{0,4},{4,8},{8,12},{12,16},{16,20},{20,24},{24,28},{28,0},{1,5},{5... | collective-permute-start | bytes 1966088 | tf_op jit(solution)/shard_map/ppermute | solution.py:34
  897.8 17.0 %collective-permute-start.2 = (f32[1280,128]{0,1:T(8,128)S(1)}, f32[1280,128]{0,1:T(8,128)S(1)}, u32[]{:S(2)}, u32[]{:S(2)}) collective-permute-start(f32[1280,128]{0,1:T(8,128)S(1)} %collective-permute-done.1), channel_id=1, source_target_pairs={{0,4},{4,8},{8,12},{12,16},{16,20},{20,24},{24,28},{28,0},{1,5},{5... | collective-permute-start | bytes 1966088 | tf_op jit(solution)/shard_map/ppermute | solution.py:34
  914.8 16.1 %collective-permute-start.3 = (f32[1280,128]{0,1:T(8,128)S(1)}, f32[1280,128]{0,1:T(8,128)S(1)}, u32[]{:S(2)}, u32[]{:S(2)}) collective-permute-start(f32[1280,128]{0,1:T(8,128)S(1)} %collective-permute-done.2), channel_id=1, source_target_pairs={{0,4},{4,8},{8,12},{12,16},{16,20},{20,24},{24,28},{28,0},{1,5},{5... | collective-permute-start | bytes 1966088 | tf_op jit(solution)/shard_map/ppermute | solution.py:34
  930.9 0.9 copy-start.5
  931.8 15.3 %collective-permute-start.4 = (f32[1280,128]{0,1:T(8,128)S(1)}, f32[1280,128]{0,1:T(8,128)S(1)}, u32[]{:S(2)}, u32[]{:S(2)}) collective-permute-start(f32[1280,128]{0,1:T(8,128)S(1)} %collective-permute-done.3), channel_id=1, source_target_pairs={{0,4},{4,8},{8,12},{12,16},{16,20},{20,24},{24,28},{28,0},{1,5},{5... | collective-permute-start | bytes 1966088 | tf_op jit(solution)/shard_map/ppermute | solution.py:34
  947.1 0.8 copy-start.7
  947.9 14.7 %collective-permute-start.5 = (f32[1280,128]{0,1:T(8,128)S(1)}, f32[1280,128]{0,1:T(8,128)}, u32[]{:S(2)}, u32[]{:S(2)}) collective-permute-start(f32[1280,128]{0,1:T(8,128)S(1)} %collective-permute-done.4), channel_id=1, source_target_pairs={{0,4},{4,8},{8,12},{12,16},{16,20},{20,24},{24,28},{28,0},{1,5},{5... | collective-permute-start | bytes 1966088 | tf_op jit(solution)/shard_map/ppermute | solution.py:34
  962.6 13.9 %collective-permute-start.6 = (f32[1280,128]{0,1:T(8,128)}, f32[1280,128]{0,1:T(8,128)}, u32[]{:S(2)}, u32[]{:S(2)}) collective-permute-start(f32[1280,128]{0,1:T(8,128)} %collective-permute-done.5), channel_id=1, source_target_pairs={{0,4},{4,8},{8,12},{12,16},{16,20},{20,24},{24,28},{28,0},{1,5},{5... | collective-permute-start | bytes 1966088 | tf_op jit(solution)/shard_map/ppermute | solution.py:34
  962.6 21.1 %copy-start.8 = (f32[1280,128]{0,1:T(8,128)S(1)}, f32[1280,128]{0,1:T(8,128)}, u32[]{:S(2)}) copy-start(f32[1280,128]{0,1:T(8,128)} %copy-done.7) | copy-start | bytes 1966084
  962.6 21.2 %copy-start.6 = (f32[1280,128]{0,1:T(8,128)S(1)}, f32[1280,128]{0,1:T(8,128)}, u32[]{:S(2)}) copy-start(f32[1280,128]{0,1:T(8,128)} %copy-done.5) | copy-start | bytes 1966084
Sparse Core Ops, SparseCore 0:
  43.8 36.0 all-reduce.3
  408.9 31.6 all-reduce.5
  696.0 31.6 all-reduce.7
Sparse Core Ops, SparseCore 1:
  73.1 105.6 reduce-scatter.6
  182.9 102.5 reduce-scatter.4
  287.9 85.2 all-gather.2
  469.7 103.0 reduce-scatter.8
  574.9 85.2 all-gather.4
  756.9 103.0 reduce-scatter.10
